TPU v7x, 32 devices: a whole 2x2x4 slice. The times are simulated.
32 devices in a mesh: ep: 4 (over y, core), etp: 8 (over z, x).
Axes of the slice: x: 2, y: 2, z: 4, core: 2. Of those that a mesh axis runs over, the one named last changes fastest.
Arguments:
- tokens: bfloat16 [4096, 7168], P(('ep', 'etp')), may hold values from -6 to 6
- expert_ids: int32 [4096, 8], P(('ep', 'etp')), may hold values from 0 to 383, all different within a row; in each aligned block of 128 rows (0 to 127, 128 to 255, ...) at most 3 rows name the same one
- gate_q: int32 [4096, 8], P(('ep', 'etp')), may hold values from 1 to 1024
- w_gate: bfloat16 [4, 7168, 2048], P('ep', None, 'etp'), may hold values from -0.0625 to 0.0625
- w_up: bfloat16 [4, 7168, 2048], P('ep', None, 'etp'), may hold values from -0.0625 to 0.0625
- w_down: bfloat16 [4, 2048, 7168], P('ep', 'etp'), may hold values from -0.125 to 0.125
Outputs:
- mixed: bfloat16 [4096, 7168], P(('ep', 'etp'))
Inputs may be any that keep to these rules, and one draw needn't show every extreme that they name: `expert_ids`: each row names 8 different experts; among the 128 rows of one device no expert is named by more than 3 rows.
All inputs are finite; a program needn't handle non-finite values.
Results may differ from a plain program's by a relative error of at most 0.014.
Values may be sent and summed in bfloat16 or wider, within the bound.
A program may use at most 64 MiB of HBM per device.

v0:
```python
import jax
import jax.numpy as jnp
from jax import lax
from jax.sharding import PartitionSpec as P

CAP = 3


def body(tokens, expert_ids, gate_q, w_gate, w_up, w_down):
    groups = lax.axis_size("ep")
    members = lax.axis_size("etp")
    capacity = CAP
    width = tokens.shape[1]
    count_rows = tokens.shape[0]
    flat_ids = expert_ids.reshape(-1)
    owner_hot = (flat_ids[:, None] == jnp.arange(groups, dtype=jnp.int32)[None, :]).astype(
        jnp.int32
    )
    earlier = jnp.cumsum(owner_hot, axis=0) - owner_hot
    position = jnp.sum(earlier * owner_hot, axis=1)
    column = jnp.where(flat_ids < groups, flat_ids * capacity + position, -1)
    select = (column[:, None] == jnp.arange(groups * capacity, dtype=jnp.int32)[None, :]).astype(
        jnp.float32
    )
    select = select.reshape(count_rows, -1, groups * capacity)
    placing = jnp.sum(select, axis=1)
    gate_scale = gate_q.astype(jnp.float32) / 1024.0
    scaling = jnp.sum(select * gate_scale[:, :, None], axis=1)
    bucket = jnp.einsum(
        "tc,td->cd", placing.astype(jnp.bfloat16), tokens, preferred_element_type=jnp.float32
    )
    bucket = bucket.astype(jnp.bfloat16).reshape(groups, capacity, width)
    gathered = lax.all_gather(bucket, "etp", axis=1, tiled=True)
    arrived = lax.all_to_all(gathered, "ep", split_axis=0, concat_axis=0, tiled=True)
    gate = jnp.dot(arrived, w_gate[0], preferred_element_type=jnp.float32)
    upper = jnp.dot(arrived, w_up[0], preferred_element_type=jnp.float32)
    hidden = (jax.nn.silu(gate) * upper).astype(jnp.bfloat16)
    inner = hidden.shape[2]
    ordered = (
        hidden.reshape(groups, members, capacity, inner).transpose(1, 0, 2, 3).reshape(-1, inner)
    )
    term = jnp.dot(ordered, w_down[0], preferred_element_type=jnp.float32)
    rounded = lax.optimization_barrier(term.astype(jnp.bfloat16))
    summed = lax.psum_scatter(
        rounded.astype(jnp.float32).astype(jnp.bfloat16), "etp", scatter_dimension=0, tiled=True
    )
    local_out = summed.reshape(groups, capacity, width)
    results = lax.all_to_all(local_out, "ep", split_axis=0, concat_axis=0, tiled=True)
    flat_out = results.reshape(groups * capacity, width).astype(jnp.float32)
    mixed = jnp.dot(scaling, flat_out, precision=lax.Precision.HIGHEST)
    return mixed.astype(jnp.bfloat16)


def solution(mesh):
    in_specs = (
        P(("ep", "etp"), None),
        P(("ep", "etp"), None),
        P(("ep", "etp"), None),
        P("ep", None, "etp"),
        P("ep", None, "etp"),
        P("ep", "etp", None),
    )
    out_specs = P(("ep", "etp"), None)
    return jax.shard_map(body, mesh=mesh, in_specs=in_specs, out_specs=out_specs, check_vma=False)
```

profile of v0, /device:TPU:0, one launch (start us, length us, event | category | flops | bytes accessed | tf_op | source)
XLA Modules:
  0.0 157.0 jit_solution(10917868213449177721)
XLA Ops:
  6.5 0.0 copy-start
  6.5 0.0 all-gather.2.cloned.1.call-start
  6.5 0.9 copy.40
  7.5 0.1 eq.43
  7.6 0.1 eq.39
  7.7 1.1 reduce-window.6
  8.8 0.2 slice_reduce_fusion
  9.0 0.2 reduce-window.9
  9.2 0.1 add_bitcast_fusion
  9.3 0.1 reduce_sum.30
  9.4 0.7 add_select_fusion
  10.2 0.7 convert_multiply_fusion
  10.9 0.0 copy-done
  10.9 0.3 convolution_convert_fusion.2
  11.2 0.1 reshape.56
  11.4 0.8 copy.43
  12.2 0.0 all-gather.2.cloned.1.call-update
  12.2 45.0 %all-gather.2.cloned.1.call-done = bf16[4,24,7168]{2,0,1:T(4,128)(2,1)} async-done(((bf16[4,3,7168]{2,0,1:T(4,128)(2,1)}), bf16[4,24,7168]{2,0,1:T(4,128)(2,1)}) %all-gather.2.cloned.1.call-update) | async-done | bytes 1376272 | tf_op jit(solution)/shard_map/all_gather | solution.py:33
  57.2 0.0 copy-start.1
  57.2 1.9 %copy.44 = bf16[4,24,7168]{2,1,0:T(8,128)(2,1)S(1)} copy(bf16[4,24,7168]{2,0,1:T(4,128)(2,1)} %all-gather.2.cloned.1.call-done) | data formatting | bytes 2752512 | tf_op jit(solution)/shard_map/all_gather | solution.py:33
  59.1 20.5 %all_to_all.10 = bf16[4,24,7168]{2,1,0:T(8,128)(2,1)S(1)} all-to-all(bf16[4,24,7168]{2,1,0:T(8,128)(2,1)S(1)} %copy.44), channel_id=1, replica_groups=mesh['ep'=4,'etp'=8] {'ep'}, dimensions={0} | all-to-all | bytes 2752512 | tf_op jit(solution)/shard_map/all_to_all | solution.py:34
  79.6 0.0 copy-done.1
  79.6 0.0 copy-start.2
  79.6 0.7 fusion.4
  80.3 1.3 copy-done.2
  81.6 0.7 fusion.9
  82.5 2.8 %convolution_convert_fusion.1 = bf16[96,7168]{1,0:T(8,128)(2,1)S(1)} fusion(bf16[96,256]{1,0:T(8,128)(2,1)S(1)} %reshape.58, bf16[1,256,7168]{2,1,0:T(8,128)(2,1)} %param.11), kind=kOutput, calls=%fused_computation.1 | convolution fusion | flops 353009664 | bytes 5095424 | tf_op jit(solution)/shard_map/dot_general | solution.py:42
  85.2 0.0 copy-start.3
  85.3 43.2 %fusion = bf16[16,7168]{1,0:T(8,128)(2,1)S(1)} fusion(bf16[96,7168]{1,0:T(8,128)(2,1)S(1)} %convolution_convert_fusion.1), kind=kCustom, calls=%all-reduce-scatter | all-reduce-scatter fusion | flops 917505 | bytes 1606144
  128.5 1.5 collective-permute-start
  130.1 0.1 slice.9
  130.1 4.1 %collective-permute-start.1 = (bf16[12,7168]{1,0:T(8,128)(2,1)S(1)}, bf16[12,7168]{1,0:T(8,128)(2,1)S(1)}, u32[]{:S(2)}, u32[]{:S(2)}) collective-permute-start(bf16[12,7168]{1,0:T(8,128)(2,1)S(1)} %slice.9), channel_id=1, source_target_pairs={{0,2},{1,3},{2,4},{3,5},{4,6},{5,7},{8,10},{9,11},{10,12},{11,13},... | collective-permute-start | bytes 516104
  134.2 0.0 copy-done.3
  134.2 0.6 dynamic-slice.4
  135.4 2.3 %collective-permute-done.1 = bf16[12,7168]{1,0:T(8,128)(2,1)S(1)} collective-permute-done((bf16[12,7168]{1,0:T(8,128)(2,1)S(1)}, bf16[12,7168]{1,0:T(8,128)(2,1)S(1)}, u32[]{:S(2)}, u32[]{:S(2)}) %collective-permute-start.1) | collective-permute-done | bytes 172064
  137.7 0.0 collective-permute-done
  137.7 1.2 concatenate
  138.9 0.1 constant_dynamic-slice_fusion
  139.0 0.1 reshape.59
  139.1 8.0 %all_to_all.11 = bf16[4,3,7168]{2,1,0:T(4,128)(2,1)S(1)} all-to-all(bf16[4,3,7168]{2,1,0:T(4,128)(2,1)S(1)} %reshape.59), channel_id=1, replica_groups=mesh['ep'=4,'etp'=8] {'ep'}, dimensions={0} | all-to-all | bytes 344064 | tf_op jit(solution)/shard_map/all_to_all | solution.py:48
  147.1 0.2 reshape.60
  147.3 2.9 %convolution_convert_fusion = bf16[128,7168]{1,0:T(8,128)(2,1)} fusion(f32[128,12]{0,1:T(8,128)S(1)} %get-tuple-element.6, bf16[12,7168]{1,0:T(8,128)(2,1)S(1)} %reshape.60), kind=kOutput, calls=%fused_computation | convolution fusion | flops 133038080 | bytes 2013184 | tf_op jit(solution)/shard_map/dot_general | solution.py:50
  (7 shorter events, 0.2 us)
Async XLA Ops:
  6.5 4.4 %copy-start = (bf16[128,7168]{1,0:T(8,128)(2,1)S(1)}, bf16[128,7168]{1,0:T(8,128)(2,1)}, u32[]{:S(2)}) copy-start(bf16[128,7168]{1,0:T(8,128)(2,1)} %param.6) | copy-start | bytes 5505028
  6.5 50.7 %all-gather.2.cloned.1.call-start = ((), (), s32[]{:S(2)}) async-start(), calls=%async_computation.2 | async-start | bytes 1548288 | tf_op jit(solution)/shard_map/all_gather | solution.py:33
  57.2 22.4 %copy-start.1 = (bf16[1,7168,256]{2,1,0:T(8,128)(2,1)S(1)}, bf16[1,7168,256]{2,1,0:T(8,128)(2,1)}, u32[]{:S(2)}) copy-start(bf16[1,7168,256]{2,1,0:T(8,128)(2,1)} %param.9) | copy-start | bytes 11010052
  79.6 2.0 %copy-start.2 = (bf16[1,7168,256]{2,1,0:T(8,128)(2,1)S(1)}, bf16[1,7168,256]{2,1,0:T(8,128)(2,1)}, u32[]{:S(2)}) copy-start(bf16[1,7168,256]{2,1,0:T(8,128)(2,1)} %param.10) | copy-start | bytes 11010052
  85.2 48.9 %copy-start.3 = (u32[32]{0:T(128)S(1)}, u32[32]{0:T(128)}, u32[]{:S(2)}) copy-start(u32[32]{0:T(128)} %constant.26) | copy-start | bytes 388
  128.5 9.2 %collective-permute-start = (bf16[16,7168]{1,0:T(8,128)(2,1)S(1)}, bf16[16,7168]{1,0:T(8,128)(2,1)S(1)}, u32[]{:S(2)}, u32[]{:S(2)}) collective-permute-start(bf16[16,7168]{1,0:T(8,128)(2,1)S(1)} %fusion), channel_id=1, source_target_pairs={{0,1},{1,2},{2,3},{3,4},{4,5},{5,6},{6,7},{8,9},{9,10},{10,11},{11... | collective-permute-start | bytes 688136
  130.1 7.6 %collective-permute-start.1 = (bf16[12,7168]{1,0:T(8,128)(2,1)S(1)}, bf16[12,7168]{1,0:T(8,128)(2,1)S(1)}, u32[]{:S(2)}, u32[]{:S(2)}) collective-permute-start(bf16[12,7168]{1,0:T(8,128)(2,1)S(1)} %slice.9), channel_id=1, source_target_pairs={{0,2},{1,3},{2,4},{3,5},{4,6},{5,7},{8,10},{9,11},{10,12},{11,13},... | collective-permute-start | bytes 516104
Sparse Core Ops, SparseCore 0:
  12.3 44.8 all-gather.1
where the time goes:
time: 157 us
  blocking collectives  71.8 us (46%)
  waiting for transfers between devices  47.3 us (30%)
  between operations  14.2 us (9%)
  local copies, waits for them, and re-layouts  7.82 us (5%)
  matrix products  7.42 us (5%)
  starting transfers between devices  5.6 us (4%)
  other arithmetic  2.87 us (2%)
    all_gather x1, waiting for transfers between devices, body(): gathered = lax.all_gather(bucket, 'etp', axis=1, tiled=True)  45 us
    unnamed x1, blocking collectives  43.2 us
    all_to_all x1, blocking collectives, body(): lax.all_to_all(gathered, 'ep', split_axis=0, concat_axis=0, tiled=True)  20.5 us
    all_to_all x1, blocking collectives, body(): lax.all_to_all(local_out, 'ep', split_axis=0, concat_axis=0, tiled=True)  8.03 us
    unnamed x2, starting transfers between devices  5.6 us
    unnamed x13, local copies, waits for them, and re-layouts  4.14 us
  transfers between devices with their start and end apart: 3, of which 2 were waited for; matrix products, arithmetic and copies ran while one was open for 0% of the time, Pallas kernels for 0%

commit v1 on v0

--- a/solution.py
+++ b/solution.py
@@ -4,6 +4,17 @@
 from jax.sharding import PartitionSpec as P
 
 CAP = 3
+
+
+def split_up(x, dim, count):
+    before, after = (x.shape[:dim], x.shape[dim + 1 :])
+    return jnp.moveaxis(x.reshape(*before, count, -1, *after), dim, 0)
+
+
+def in_order(blocks, dim):
+    shape = list(blocks.shape[1:])
+    shape[dim] *= blocks.shape[0]
+    return jnp.moveaxis(blocks, 0, dim).reshape(shape)
 
 
 def body(tokens, expert_ids, gate_q, w_gate, w_up, w_down):
@@ -45,7 +56,14 @@
         rounded.astype(jnp.float32).astype(jnp.bfloat16), "etp", scatter_dimension=0, tiled=True
     )
     local_out = summed.reshape(groups, capacity, width)
-    results = lax.all_to_all(local_out, "ep", split_axis=0, concat_axis=0, tiled=True)
+    size, index = (lax.axis_size("ep"), lax.axis_index("ep"))
+    blocks = split_up(local_out, 0, size)
+    outs = [blocks[index]]
+    for turn in range(1, size):
+        sent = blocks[index ^ turn]
+        outs.append(lax.ppermute(sent, "ep", [(i, i ^ turn) for i in range(size)]))
+    blocks = jnp.stack(outs)[index ^ jnp.arange(size)]
+    results = in_order(blocks, 0)
     flat_out = results.reshape(groups * capacity, width).astype(jnp.float32)
     mixed = jnp.dot(scaling, flat_out, precision=lax.Precision.HIGHEST)
     return mixed.astype(jnp.bfloat16)

time: 157 us -> 155 us (0.987)
  blocking collectives: 71.8 us -> 63.7 us
  waiting for transfers between devices: 47.3 us -> 50.2 us
  starting transfers between devices: 5.6 us -> 7.51 us
    all_to_all x1 -> x0, blocking collectives: 8.03 us -> none  [body(): lax.all_to_all(local_out, 'ep', split_axis=0, concat_axis=0, tiled=True)]
    ppermute x0 -> x3, waiting for transfers between devices: none -> 2.97 us  [body(): outs.append(lax.ppermute(sent, 'ep', [(i, i ^ turn) for i in range(size)]))]
    ppermute x0 -> x3, starting transfers between devices: none -> 1.91 us  [body(): outs.append(lax.ppermute(sent, 'ep', [(i, i ^ turn) for i in range(size)]))]
  transfers between devices with their start and end apart: 3 -> 6, of which waited for: 2 -> 4; matrix products, arithmetic and copies ran while one was open for 0% -> 0% of each run, Pallas kernels for 0% -> 0%
where the time goes in v1:
time: 155 us
  blocking collectives  63.7 us (41%)
  waiting for transfers between devices  50.2 us (32%)
  between operations  14.3 us (9%)
  local copies, waits for them, and re-layouts  8.66 us (6%)
  starting transfers between devices  7.51 us (5%)
  matrix products  7.42 us (5%)
  other arithmetic  3.09 us (2%)
    all_gather x1, waiting for transfers between devices, body(): gathered = lax.all_gather(bucket, 'etp', axis=1, tiled=True)  45 us
    unnamed x1, blocking collectives  43.2 us
    all_to_all x1, blocking collectives, body(): lax.all_to_all(gathered, 'ep', split_axis=0, concat_axis=0, tiled=True)  20.5 us
    unnamed x2, starting transfers between devices  5.6 us
    unnamed x13, local copies, waits for them, and re-layouts  4.14 us
  transfers between devices with their start and end apart: 6, of which 4 were waited for; matrix products, arithmetic and copies ran while one was open for 0% of the time, Pallas kernels for 0%

profile of v1, /device:TPU:0, one launch (start us, length us, event | category | flops | bytes accessed | tf_op | source)
XLA Modules:
  0.0 154.9 jit_solution(2643849074247078757)
XLA Ops:
  6.5 0.0 copy-start
  6.5 0.0 all-gather.2.cloned.1.call-start
  6.5 0.9 copy.40
  7.5 0.1 eq.43
  7.6 0.1 eq.39
  7.7 1.1 reduce-window.6
  8.8 0.2 slice_reduce_fusion
  9.0 0.2 reduce-window.9
  9.2 0.1 add_bitcast_fusion
  9.3 0.1 reduce_sum.30
  9.4 0.7 add_select_fusion
  10.2 0.7 convert_multiply_fusion
  10.9 0.0 copy-done
  10.9 0.3 convolution_convert_fusion.2
  11.2 0.1 reshape.66
  11.4 0.8 copy.43
  12.2 0.0 all-gather.2.cloned.1.call-update
  12.2 45.0 %all-gather.2.cloned.1.call-done = bf16[4,24,7168]{2,0,1:T(4,128)(2,1)} async-done(((bf16[4,3,7168]{2,0,1:T(4,128)(2,1)}), bf16[4,24,7168]{2,0,1:T(4,128)(2,1)}) %all-gather.2.cloned.1.call-update) | async-done | bytes 1376272 | tf_op jit(solution)/shard_map/all_gather | solution.py:44
  57.2 0.0 copy-start.1
  57.2 1.9 %copy.44 = bf16[4,24,7168]{2,1,0:T(8,128)(2,1)S(1)} copy(bf16[4,24,7168]{2,0,1:T(4,128)(2,1)} %all-gather.2.cloned.1.call-done) | data formatting | bytes 2752512 | tf_op jit(solution)/shard_map/all_gather | solution.py:44
  59.1 20.5 %all_to_all.5 = bf16[4,24,7168]{2,1,0:T(8,128)(2,1)S(1)} all-to-all(bf16[4,24,7168]{2,1,0:T(8,128)(2,1)S(1)} %copy.44), channel_id=1, replica_groups=mesh['ep'=4,'etp'=8] {'ep'}, dimensions={0} | all-to-all | bytes 2752512 | tf_op jit(solution)/shard_map/all_to_all | solution.py:45
  79.6 0.0 copy-done.1
  79.6 0.0 copy-start.2
  79.6 0.7 fusion.4
  80.3 1.3 copy-done.2
  81.6 0.7 fusion.9
  82.5 2.8 %convolution_convert_fusion.1 = bf16[96,7168]{1,0:T(8,128)(2,1)S(1)} fusion(bf16[96,256]{1,0:T(8,128)(2,1)S(1)} %reshape.68, bf16[1,256,7168]{2,1,0:T(8,128)(2,1)} %param.11), kind=kOutput, calls=%fused_computation.2 | convolution fusion | flops 353009664 | bytes 5095424 | tf_op jit(solution)/shard_map/dot_general | solution.py:53
  85.2 0.0 copy-start.3
  85.3 43.2 %fusion = bf16[16,7168]{1,0:T(8,128)(2,1)S(1)} fusion(bf16[96,7168]{1,0:T(8,128)(2,1)S(1)} %convolution_convert_fusion.1), kind=kCustom, calls=%all-reduce-scatter | all-reduce-scatter fusion | flops 917505 | bytes 1606144
  128.5 1.5 collective-permute-start.3
  130.1 0.1 slice.11
  130.1 4.1 %collective-permute-start.4 = (bf16[12,7168]{1,0:T(8,128)(2,1)S(1)}, bf16[12,7168]{1,0:T(8,128)(2,1)S(1)}, u32[]{:S(2)}, u32[]{:S(2)}) collective-permute-start(bf16[12,7168]{1,0:T(8,128)(2,1)S(1)} %slice.11), channel_id=1, source_target_pairs={{0,2},{1,3},{2,4},{3,5},{4,6},{5,7},{8,10},{9,11},{10,12},{11,13},... | collective-permute-start | bytes 516104
  134.2 0.0 copy-done.3
  134.2 0.6 dynamic-slice.4
  135.5 2.2 %collective-permute-done.4 = bf16[12,7168]{1,0:T(8,128)(2,1)S(1)} collective-permute-done((bf16[12,7168]{1,0:T(8,128)(2,1)S(1)}, bf16[12,7168]{1,0:T(8,128)(2,1)S(1)}, u32[]{:S(2)}, u32[]{:S(2)}) %collective-permute-start.4) | collective-permute-done | bytes 172064
  137.7 0.0 collective-permute-done.3
  137.7 1.2 concatenate
  138.9 0.1 constant_dynamic-slice_fusion
  139.0 0.1 reshape_reshape.6
  139.1 0.1 constant_dynamic-slice_fusion.1
  139.2 0.1 collective-permute-start.2
  139.3 0.1 collective-permute-start.1
  139.4 1.8 %collective-permute-start = (bf16[1,3,7168]{2,1,0:T(4,128)(2,1)S(1)}, bf16[1,3,7168]{2,1,0:T(4,128)(2,1)S(1)}, u32[]{:S(2)}, u32[]{:S(2)}) collective-permute-start(bf16[1,3,7168]{2,1,0:T(4,128)(2,1)S(1)} %get-tuple-element.10), channel_id=1, source_target_pairs={{0,8},{8,0},{16,24},{24,16},{1,9},{9,1},{17,25},{25,17},{2,10},{10... | collective-permute-start | bytes 129032 | tf_op jit(solution)/shard_map/ppermute | solution.py:64
  141.1 1.7 %collective-permute-done.2 = bf16[1,3,7168]{2,1,0:T(4,128)(2,1)S(1)} collective-permute-done((bf16[1,3,7168]{2,1,0:T(4,128)(2,1)S(1)}, bf16[1,3,7168]{2,1,0:T(4,128)(2,1)S(1)}, u32[]{:S(2)}, u32[]{:S(2)}) %collective-permute-start.2) | collective-permute-done | bytes 43040 | tf_op jit(solution)/shard_map/ppermute | solution.py:64
  142.9 1.2 collective-permute-done.1
  144.1 0.0 collective-permute-done
  144.1 0.2 maximum_bitcast_fusion
  144.3 0.7 gather_fusion
  145.1 0.2 reshape_reshape.7
  145.2 2.9 %convolution_convert_fusion = bf16[128,7168]{1,0:T(8,128)(2,1)} fusion(f32[128,12]{0,1:T(8,128)S(1)} %get-tuple-element.6, bf16[12,7168]{1,0:T(8,128)(2,1)S(1)} %reshape_reshape.7), kind=kOutput, calls=%fused_computation.1 | convolution fusion | flops 133038080 | bytes 2013184 | tf_op jit(solution)/shard_map/dot_general | solution.py:68
  (9 shorter events, 0.2 us)
Async XLA Ops:
  6.5 4.4 %copy-start = (bf16[128,7168]{1,0:T(8,128)(2,1)S(1)}, bf16[128,7168]{1,0:T(8,128)(2,1)}, u32[]{:S(2)}) copy-start(bf16[128,7168]{1,0:T(8,128)(2,1)} %param.6) | copy-start | bytes 5505028
  6.5 50.7 %all-gather.2.cloned.1.call-start = ((), (), s32[]{:S(2)}) async-start(), calls=%async_computation.1 | async-start | bytes 1548288 | tf_op jit(solution)/shard_map/all_gather | solution.py:44
  57.2 22.4 %copy-start.1 = (bf16[1,7168,256]{2,1,0:T(8,128)(2,1)S(1)}, bf16[1,7168,256]{2,1,0:T(8,128)(2,1)}, u32[]{:S(2)}) copy-start(bf16[1,7168,256]{2,1,0:T(8,128)(2,1)} %param.9) | copy-start | bytes 11010052
  79.6 2.0 %copy-start.2 = (bf16[1,7168,256]{2,1,0:T(8,128)(2,1)S(1)}, bf16[1,7168,256]{2,1,0:T(8,128)(2,1)}, u32[]{:S(2)}) copy-start(bf16[1,7168,256]{2,1,0:T(8,128)(2,1)} %param.10) | copy-start | bytes 11010052
  85.2 49.0 %copy-start.3 = (u32[32]{0:T(128)S(1)}, u32[32]{0:T(128)}, u32[]{:S(2)}) copy-start(u32[32]{0:T(128)} %constant.39) | copy-start | bytes 388
  128.5 9.2 %collective-permute-start.3 = (bf16[16,7168]{1,0:T(8,128)(2,1)S(1)}, bf16[16,7168]{1,0:T(8,128)(2,1)S(1)}, u32[]{:S(2)}, u32[]{:S(2)}) collective-permute-start(bf16[16,7168]{1,0:T(8,128)(2,1)S(1)} %fusion), channel_id=1, source_target_pairs={{0,1},{1,2},{2,3},{3,4},{4,5},{5,6},{6,7},{8,9},{9,10},{10,11},{11... | collective-permute-start | bytes 688136
  130.1 7.6 %collective-permute-start.4 = (bf16[12,7168]{1,0:T(8,128)(2,1)S(1)}, bf16[12,7168]{1,0:T(8,128)(2,1)S(1)}, u32[]{:S(2)}, u32[]{:S(2)}) collective-permute-start(bf16[12,7168]{1,0:T(8,128)(2,1)S(1)} %slice.11), channel_id=1, source_target_pairs={{0,2},{1,3},{2,4},{3,5},{4,6},{5,7},{8,10},{9,11},{10,12},{11,13},... | collective-permute-start | bytes 516104
  139.2 3.7 %collective-permute-start.2 = (bf16[1,3,7168]{2,1,0:T(4,128)(2,1)S(1)}, bf16[1,3,7168]{2,1,0:T(4,128)(2,1)S(1)}, u32[]{:S(2)}, u32[]{:S(2)}) collective-permute-start(bf16[1,3,7168]{2,1,0:T(4,128)(2,1)S(1)} %get-tuple-element.8), channel_id=1, source_target_pairs={{0,24},{8,16},{16,8},{24,0},{1,25},{9,17},{17,9},{25,1},{2,26},{10... | collective-permute-start | bytes 129032 | tf_op jit(solution)/shard_map/ppermute | solution.py:64
  139.3 4.8 %collective-permute-start.1 = (bf16[1,3,7168]{2,1,0:T(4,128)(2,1)S(1)}, bf16[1,3,7168]{2,1,0:T(4,128)(2,1)S(1)}, u32[]{:S(2)}, u32[]{:S(2)}) collective-permute-start(bf16[1,3,7168]{2,1,0:T(4,128)(2,1)S(1)} %get-tuple-element.9), channel_id=1, source_target_pairs={{0,16},{8,24},{16,0},{24,8},{1,17},{9,25},{17,1},{25,9},{2,18},{10... | collective-permute-start | bytes 129032 | tf_op jit(solution)/shard_map/ppermute | solution.py:64
  139.4 4.7 %collective-permute-start = (bf16[1,3,7168]{2,1,0:T(4,128)(2,1)S(1)}, bf16[1,3,7168]{2,1,0:T(4,128)(2,1)S(1)}, u32[]{:S(2)}, u32[]{:S(2)}) collective-permute-start(bf16[1,3,7168]{2,1,0:T(4,128)(2,1)S(1)} %get-tuple-element.10), channel_id=1, source_target_pairs={{0,8},{8,0},{16,24},{24,16},{1,9},{9,1},{17,25},{25,17},{2,10},{10... | collective-permute-start | bytes 129032 | tf_op jit(solution)/shard_map/ppermute | solution.py:64
Sparse Core Ops, SparseCore 0:
  12.3 44.8 all-gather.1
